TPU v7x, 32 devices: a whole 2x2x4 slice. The times are simulated.
32 devices in a mesh: seq: 8 (over y, x, core), head: 4 (over z).
Axes of the slice: x: 2, y: 2, z: 4, core: 2. Of those that a mesh axis runs over, the one named last changes fastest.
Arguments:
- key_rows: bfloat16 [2048, 2048], P('seq', 'head'), may hold values from -1 to 1, as said below
- values: bfloat16 [2048, 2048], P('seq', 'head'), may hold values from -6 to 6
- d_layer: bfloat16 [2048, 2048], P('seq', 'head'), may hold values from -6 to 6
- out_weight: bfloat16 [2048, 2048], P('head'), may hold values from -0.125 to 0.125
- saved_solutions: float32 [2048, 2048], P('seq', 'head'), may hold values from -0.625 to 0.625
- ridge_scale: float32 [16], P('head'), may hold values from 0.5 to 4
Outputs:
- grad_queries: float32 [2048, 2048], P('seq', 'head')
- grad_keys: float32 [2048, 2048], P('seq', 'head')
- grad_values: float32 [2048, 2048], P('seq', 'head')
Inputs may be any that keep to these rules, and one draw needn't show every extreme that they name: `key_rows`: within each head the 128 entries of a key have Euclidean norm 1 up to bfloat16 rounding.
All inputs are finite; a program needn't handle non-finite values.
Results may differ from a plain program's by a relative error of at most 0.0029.
Values may be sent and summed in bfloat16 or wider, within the bound.
A program may use at most 64 MiB of HBM per device.

v0:
```python
import functools
import jax
import jax.numpy as jnp
from jax import lax
from jax.experimental import pallas as pl
from jax.experimental.pallas import tpu as pltpu
from jax.sharding import PartitionSpec as P

DH = 128
ITERS = 8
EPSILON = 1e-06
BF = jnp.bfloat16
F32 = jnp.float32

def nn(left, right):
    return lax.dot_general(left, right, (((1,), (0,)), ((), ())), preferred_element_type=F32)


def nt(left, right):
    return lax.dot_general(left, right, (((1,), (1,)), ((), ())), preferred_element_type=F32)


def split(a):
    hi = a.astype(BF)
    return hi, (a - hi.astype(F32)).astype(BF)


def flip(a):
    return a.astype(F32).T.astype(BF)


def head(ref, h):
    return ref[:, h * DH : (h + 1) * DH]


def window_masked(scores):
    tok = scores.shape[1]
    key_ids = lax.broadcasted_iota(jnp.int32, (tok, tok), 0)
    tok_ids = lax.broadcasted_iota(jnp.int32, (tok, tok), 1)
    own = key_ids <= tok_ids
    return jnp.concatenate(
        [jnp.where(own, scores[:tok], 0.0), jnp.where(own, 0.0, scores[tok:])], axis=0
    )


def rows_sum(ref, h):
    total = None
    for slot in range(ref.shape[0]):
        part = ref[slot, h].astype(F32)
        total = part if total is None else total + part
    return total


def own_kernel(key, val, sol, sav, out, gk, gv):
    tok = key.shape[0]
    key_ids = lax.broadcasted_iota(jnp.int32, (tok, tok), 0)
    tok_ids = lax.broadcasted_iota(jnp.int32, (tok, tok), 1)
    later = tok_ids >= key_ids
    for h in range(key.shape[1] // DH):
        k, v, o = head(key, h), head(val, h), head(out, h)
        x_hi, x_lo = split(head(sav, h))
        y_hi, y_lo = split(-head(sol, h))
        a1 = nt(jnp.concatenate([k, k], axis=1), jnp.concatenate([x_hi, x_lo], axis=1))
        a2 = nt(jnp.concatenate([v, k], axis=1), jnp.concatenate([o, y_hi], axis=1)) + nt(k, y_lo)
        a1_hi, a1_lo = split(jnp.where(later, a1, 0.0))
        a2_hi, a2_lo = split(jnp.where(later, a2, 0.0))
        yo = jnp.concatenate([y_hi, o], axis=1)
        both = nn(a1_hi, yo) + nn(a1_lo, yo)
        g = both[:, :DH] + nn(a1_hi, y_lo) + nn(a2_hi, x_hi) + nn(a2_lo, x_hi) + nn(a2_hi, x_lo)
        gk[:, h * DH : (h + 1) * DH] = g
        gv[:, h * DH : (h + 1) * DH] = both[:, DH:]


def lead_kernel(key, val, sol, sav, out, pair, cross, gk_own, gv_own, gk, gv):
    tok = key.shape[0]
    key_ids = lax.broadcasted_iota(jnp.int32, (tok, tok), 0)
    tok_ids = lax.broadcasted_iota(jnp.int32, (tok, tok), 1)
    later = tok_ids < key_ids
    for h in range(key.shape[1] // DH):
        k, v, o, x, y = head(key, h), head(val, h), head(out, h), head(sav, h), -head(sol, h)
        vk = jnp.concatenate([v, k], axis=1)
        a1_hi, a1_lo = split(jnp.where(later, nt(k, x), 0.0))
        a2_hi, a2_lo = split(jnp.where(later, nt(vk, jnp.concatenate([o, y], axis=1)), 0.0))
        yo = jnp.concatenate([y, o], axis=1)
        c_hi, c_lo = split(rows_sum(cross, h))
        p_hi, p_lo = split(-rows_sum(pair, h))
        both = nn(a1_hi, yo) + nn(a1_lo, yo)
        both = both + nn(k, jnp.concatenate([p_hi, c_hi], axis=1)) + nn(k, jnp.concatenate([p_lo, c_lo], axis=1))
        g = both[:, :DH] + nn(a2_hi, x) + nn(a2_lo, x)
        g = g + nt(vk, jnp.concatenate([c_hi, p_hi], axis=1)) + nt(vk, jnp.concatenate([c_lo, p_lo], axis=1))
        at = slice(h * DH, (h + 1) * DH)
        gk[:, at] = gk_own[:, at] + g
        gv[:, at] = gv_own[:, at] + both[:, DH:]


def mega(span, n_seq, n_head, ridge, key, val, d_own, w_hbm, sav_hbm, sol, gk, gv,
         w, sav, sav_bf, out, sol_bf, gram, state, cross, pair,
         d_in, key_lag, val_lag, sav_lead, out_lead, sol_lead, gram_in, state_in, cross_in, pair_in,
         r_s, p_s, y_s, rr_s, k2_s, kt_s, g_s, local_sem, send_sem, recv_sem):
    s = lax.axis_index("seq")
    me = lax.axis_index("head")
    heads = gram.shape[0]
    tok = key.shape[0]
    w_copy = pltpu.make_async_copy(w_hbm, w, local_sem.at[0])
    x_copy = pltpu.make_async_copy(sav_hbm, sav, local_sem.at[1])
    w_copy.start()
    x_copy.start()

    offsets = [d for m in range(1, span + 1) for d in (m, -m)]

    def exists(d):
        return s + d < n_seq if d > 0 else s + d >= 0

    barrier = pltpu.get_barrier_semaphore()
    for j in range(1, n_head):
        pl.semaphore_signal(
            barrier, inc=1, device_id={"head": lax.rem(me + j, n_head)}, device_id_type=pl.DeviceIdType.MESH
        )
    for d in offsets:
        @pl.when(exists(d))
        def _():
            pl.semaphore_signal(barrier, inc=1, device_id={"seq": s + d}, device_id_type=pl.DeviceIdType.MESH)
    pl.semaphore_wait(
        barrier, n_head - 1 + jnp.minimum(s, span) + jnp.minimum(n_seq - 1 - s, span)
    )

    counter = [0]
    sends = []

    class Hop:
        def __init__(self, source, target, d):
            self.d = d
            self.copy = pltpu.make_async_remote_copy(
                src_ref=source,
                dst_ref=target,
                send_sem=send_sem.at[counter[0]],
                recv_sem=recv_sem.at[counter[0]],
                device_id={"seq": s + d},
                device_id_type=pl.DeviceIdType.MESH,
            )
            counter[0] += 1
            sends.append(self)

            @pl.when(jnp.logical_not(exists(-d)))
            def _():
                target[...] = jnp.zeros(target.shape, target.dtype)

        def start(self):
            pl.when(exists(self.d))(self.copy.start)
            return self

        def arrive(self):
            pl.when(exists(-self.d))(self.copy.wait_recv)

        def finish(self):
            pl.when(exists(self.d))(self.copy.wait_send)

    def mids(source, target, sign):
        return [Hop(source, target.at[m - 1], sign * m).start() for m in range(1, span)]

    key_hop = Hop(key, key_lag, span).start()
    d_copies = []
    for j in range(1, n_head):
        copy = pltpu.make_async_remote_copy(
            src_ref=d_own,
            dst_ref=d_in.at[j - 1],
            send_sem=send_sem.at[counter[0]],
            recv_sem=recv_sem.at[counter[0]],
            device_id={"head": lax.rem(me + j, n_head)},
            device_id_type=pl.DeviceIdType.MESH,
        )
        counter[0] += 1
        copy.start()
        d_copies.append(copy)
    val_hop = Hop(val, val_lag, span).start()

    for h in range(heads):
        k = head(key, h)
        both = nn(flip(k), jnp.concatenate([k, head(val, h)], axis=1)).astype(BF)
        gram[h] = both[:, :DH]
        state[h] = both[:, DH:]
    state_hops = mids(state, state_in, 1)
    gram_hops = mids(gram, gram_in, 1)
    x_copy.wait()
    sav_bf[...] = sav[...].astype(BF)
    sav_hop = Hop(sav_bf, sav_lead, -span).start()

    w_copy.wait()
    width = d_own.shape[1]
    acc = None
    for j in range(n_head):
        if j:
            d_copies[j - 1].wait_recv()
        piece = d_own[...] if j == 0 else d_in[j - 1]
        col = lax.rem(me + (n_head - j), n_head) * width
        part = nt(piece, w[:, pl.ds(pl.multiple_of(col, width), width)])
        acc = part if acc is None else acc + part
    out[...] = acc.astype(BF)
    out_hop = Hop(out, out_lead, -span).start()
    for h in range(heads):
        x_hi, x_lo = split(head(sav, h).T)
        o = head(out, h)
        cross[h] = (nn(x_hi, o) + nn(x_lo, o)).astype(BF)
    cross_hops = mids(cross, cross_in, -1)

    key_hop.arrive()
    for h in range(heads):
        k_cat = jnp.concatenate([head(key, h), head(key_lag, h)], axis=0)
        k2_s[h] = jnp.concatenate([k_cat, k_cat], axis=1)
        kt_s[h] = flip(k_cat)
    val_hop.arrive()
    for hop in state_hops + gram_hops:
        hop.arrive()
    for h in range(heads):
        o = head(out, h)
        v_cat = jnp.concatenate([head(val, h), head(val_lag, h)], axis=0)
        s_hi, s_lo = split(window_masked(nt(v_cat, o)))
        st_hi, st_lo = split(rows_sum(state_in, h))
        r = nn(kt_s[h], s_hi) + nn(kt_s[h], s_lo) + nt(st_hi, o) + nt(st_lo, o)
        g_hi, g_lo = split(rows_sum(gram_in, h))
        g_s[h] = jnp.concatenate([g_hi, g_hi, g_lo], axis=1)
        r_s[h] = r
        p_s[h] = r
        y_s[h] = jnp.zeros_like(r)
        rr_s[h] = jnp.sum(r * r, axis=0, keepdims=True)

    def step(_, carry):
        for h in range(heads):
            p = p_s[h]
            p_hi, p_lo = split(p)
            scores = nn(k2_s[h], jnp.concatenate([p_hi, p_lo], axis=0))
            masked = window_masked(scores).astype(BF)
            image = nn(kt_s[h], masked) + nn(g_s[h], jnp.concatenate([p_hi, p_lo, p_hi], axis=0))
            image = image + ridge[h] * p
            rr = rr_s[h]
            alpha = rr / (jnp.sum(p * image, axis=0, keepdims=True) + EPSILON)
            y_s[h] = y_s[h] + alpha * p
            r = r_s[h] - alpha * image
            r_s[h] = r
            nr = jnp.sum(r * r, axis=0, keepdims=True)
            p_s[h] = r + nr / (rr + EPSILON) * p
            rr_s[h] = nr
        return carry

    lax.fori_loop(0, ITERS, step, 0)
    for h in range(heads):
        y = y_s[h].T
        sol[:, h * DH : (h + 1) * DH] = y
        sol_bf[:, h * DH : (h + 1) * DH] = y.astype(BF)
    sol_hop = Hop(sol_bf, sol_lead, -span).start()
    for h in range(heads):
        y_hi, y_lo = split(head(sol, h))
        x_hi, x_lo = split(head(sav, h).T)
        pair[h] = (nn(x_hi, y_hi) + nn(x_lo, y_hi) + nn(x_hi, y_lo)).astype(BF)
    pair_hops = mids(pair, pair_in, -1)

    own_kernel(key, val, sol, sav, out, gk, gv)
    for hop in [sav_hop, out_hop] + cross_hops + [sol_hop] + pair_hops:
        hop.arrive()
    lead_kernel(key, val, sol_lead, sav_lead, out_lead, pair_in, cross_in, gk, gv, gk, gv)
    for copy in d_copies:
        copy.wait_send()
    for hop in sends:
        hop.finish()


def body(key_rows, values, d_layer, out_weight, saved_solutions, ridge_scale):
    tok, cols = key_rows.shape
    heads = cols // DH
    n_seq, n_head = lax.axis_size("seq"), lax.axis_size("head")
    span = n_seq // 4
    slots = max(span - 1, 1)
    copies = n_head - 1 + 5 + 4 * (span - 1)
    vmem = pl.BlockSpec(memory_space=pltpu.VMEM)
    smem = pl.BlockSpec(memory_space=pltpu.SMEM)
    hbm = pl.BlockSpec(memory_space=pl.ANY)
    flat = jax.ShapeDtypeStruct((tok, cols), F32)
    half = pltpu.VMEM((tok, cols), BF)
    mats = pltpu.VMEM((heads, DH, DH), BF)
    mats_in = pltpu.VMEM((slots, heads, DH, DH), BF)
    vec = pltpu.VMEM((heads, DH, tok), F32)
    return pl.pallas_call(
        functools.partial(mega, span, n_seq, n_head),
        name="layer",
        out_shape=[flat, flat, flat],
        in_specs=[smem, vmem, vmem, vmem, hbm, hbm],
        out_specs=[vmem, vmem, vmem],
        scratch_shapes=[
            pltpu.VMEM(out_weight.shape, BF), pltpu.VMEM((tok, cols), F32), half, half, half,
            mats, mats, mats, mats,
            pltpu.VMEM((n_head - 1,) + d_layer.shape, BF), half, half, half, half, half,
            mats_in, mats_in, mats_in, mats_in,
            vec, vec, vec,
            pltpu.VMEM((heads, 1, tok), F32),
            pltpu.VMEM((heads, 2 * tok, 2 * DH), BF),
            pltpu.VMEM((heads, DH, 2 * tok), BF),
            pltpu.VMEM((heads, DH, 3 * DH), BF),
            pltpu.SemaphoreType.DMA((2,)),
            pltpu.SemaphoreType.DMA((copies,)),
            pltpu.SemaphoreType.DMA((copies,)),
        ],
        compiler_params=pltpu.CompilerParams(
            collective_id=0, has_side_effects=True, vmem_limit_bytes=40 << 20
        ),
    )(ridge_scale, key_rows, values, d_layer, out_weight, saved_solutions)


def solution(mesh):
    return jax.shard_map(
        body,
        mesh=mesh,
        in_specs=(
            P("seq", "head"),
            P("seq", "head"),
            P("seq", "head"),
            P("head", None),
            P("seq", "head"),
            P("head"),
        ),
        out_specs=(P("seq", "head"), P("seq", "head"), P("seq", "head")),
        check_vma=False,
    )
```

profile of v0, /device:TPU:11, one launch (start us, length us, event | category | flops | bytes accessed | tf_op | source)
XLA Modules:
  0.0 57.7 jit_solution(8378344508273113067)
XLA Ops:
  0.6 0.0 copy-start
  0.6 1.6 %copy-done = bf16[512,2048]{1,0:T(8,128)(2,1)S(1)} copy-done((bf16[512,2048]{1,0:T(8,128)(2,1)S(1)}, bf16[512,2048]{1,0:T(8,128)(2,1)}, u32[]{:S(2)}) %copy-start) | copy-done | bytes 2097176
  2.2 0.0 copy-start.1
  2.2 1.0 %copy-done.1 = f32[256,512]{1,0:T(8,128)S(1)} copy-done((f32[256,512]{1,0:T(8,128)S(1)}, f32[256,512]{1,0:T(8,128)}, u32[]{:S(2)}) %copy-start.1) | copy-done | bytes 524312
  3.3 0.0 copy-start.2
  3.3 0.9 %copy-done.2 = bf16[256,512]{1,0:T(8,128)(2,1)S(1)} copy-done((bf16[256,512]{1,0:T(8,128)(2,1)S(1)}, bf16[256,512]{1,0:T(8,128)(2,1)}, u32[]{:S(2)}) %copy-start.2) | copy-done | bytes 262168
  4.2 0.0 copy-start.3
  4.2 0.9 %copy-done.3 = bf16[256,512]{1,0:T(8,128)(2,1)S(1)} copy-done((bf16[256,512]{1,0:T(8,128)(2,1)S(1)}, bf16[256,512]{1,0:T(8,128)(2,1)}, u32[]{:S(2)}) %copy-start.3) | copy-done | bytes 262168
  5.2 0.0 copy-start.4
  5.2 0.9 %copy-done.4 = bf16[256,512]{1,0:T(8,128)(2,1)S(1)} copy-done((bf16[256,512]{1,0:T(8,128)(2,1)S(1)}, bf16[256,512]{1,0:T(8,128)(2,1)}, u32[]{:S(2)}) %copy-start.4) | copy-done | bytes 262168
  6.1 0.0 copy-start.5
  6.1 0.7 %copy-done.5 = f32[4]{0:T(128)S(1)} copy-done((f32[4]{0:T(128)S(1)}, f32[4]{0:T(128)}, u32[]{:S(2)}) %copy-start.5) | copy-done | bytes 40
  6.8 48.5 %layer.1 = (f32[256,512]{1,0:T(8,128)S(1)}, f32[256,512]{1,0:T(8,128)S(1)}, f32[256,512]{1,0:T(8,128)S(1)}) custom-call(f32[4]{0:T(128)S(1)} %copy-done.5, bf16[256,512]{1,0:T(8,128)(2,1)S(1)} %copy-done.2, bf16[256,512]{1,0:T(8,128)(2,1)S(1)} %copy-done.3, bf16[256,512]{1,0:T(8,128)(2,1)S(1)} %copy-done.4, bf16[512,2048]{1,0:T(8,128)(2,1)S(1)} %copy-done, ...), custom_call_target="tpu_custom_call" | custom-call | tf_op jit(solution)/shard_map/layer/pallas_call | solution.py:282
  55.3 0.8 %copy.12 = f32[256,512]{1,0:T(8,128)} copy(f32[256,512]{1,0:T(8,128)S(1)} %get-tuple-element.6) | data formatting | bytes 1048576
  56.1 0.8 %copy.13 = f32[256,512]{1,0:T(8,128)} copy(f32[256,512]{1,0:T(8,128)S(1)} %get-tuple-element.7) | data formatting | bytes 1048576
  56.9 0.8 %copy.14 = f32[256,512]{1,0:T(8,128)} copy(f32[256,512]{1,0:T(8,128)S(1)} %get-tuple-element.8) | data formatting | bytes 1048576
Async XLA Ops:
  0.6 1.6 %copy-start = (bf16[512,2048]{1,0:T(8,128)(2,1)S(1)}, bf16[512,2048]{1,0:T(8,128)(2,1)}, u32[]{:S(2)}) copy-start(bf16[512,2048]{1,0:T(8,128)(2,1)} %w_hbm.1) | copy-start | bytes 6291460
  2.2 1.0 %copy-start.1 = (f32[256,512]{1,0:T(8,128)S(1)}, f32[256,512]{1,0:T(8,128)}, u32[]{:S(2)}) copy-start(f32[256,512]{1,0:T(8,128)} %sav_hbm.1) | copy-start | bytes 1572868
  3.3 0.9 %copy-start.2 = (bf16[256,512]{1,0:T(8,128)(2,1)S(1)}, bf16[256,512]{1,0:T(8,128)(2,1)}, u32[]{:S(2)}) copy-start(bf16[256,512]{1,0:T(8,128)(2,1)} %key.1) | copy-start | bytes 786436
  4.2 0.9 %copy-start.3 = (bf16[256,512]{1,0:T(8,128)(2,1)S(1)}, bf16[256,512]{1,0:T(8,128)(2,1)}, u32[]{:S(2)}) copy-start(bf16[256,512]{1,0:T(8,128)(2,1)} %val.1) | copy-start | bytes 786436
  5.2 0.9 %copy-start.4 = (bf16[256,512]{1,0:T(8,128)(2,1)S(1)}, bf16[256,512]{1,0:T(8,128)(2,1)}, u32[]{:S(2)}) copy-start(bf16[256,512]{1,0:T(8,128)(2,1)} %d_own.1) | copy-start | bytes 786436
  6.1 0.7 %copy-start.5 = (f32[4]{0:T(128)S(1)}, f32[4]{0:T(128)}, u32[]{:S(2)}) copy-start(f32[4]{0:T(128)} %ridge.1) | copy-start | bytes 52
where the time goes:
time: 58 us; the launch traced here: 57.7 us
  Pallas kernels  48.5 us (84%)
  local copies, waits for them, and re-layouts  8.51 us (15%)
  between operations  0.65 us (1%)
    pallas_call x1, Pallas kernels, body(): pl.pallas_call(functools.partial(mega, span, n_seq, n_head), name='layer'...  48.5 us
    unnamed x15, local copies, waits for them, and re-layouts  8.51 us

commit v1 on v0

--- a/solution.py
+++ b/solution.py
@@ -93,8 +93,8 @@
         gv[:, at] = gv_own[:, at] + both[:, DH:]
 
 
-def mega(span, n_seq, n_head, ridge, key, val, d_own, w_hbm, sav_hbm, sol, gk, gv,
-         w, sav, sav_bf, out, sol_bf, gram, state, cross, pair,
+def mega(span, n_seq, n_head, ridge, key_hbm, val_hbm, d_hbm, w_hbm, sav_hbm, sol, gk, gv,
+         key, val, d_own, w, sav, sav_bf, out, sol_bf, gram, state, cross, pair,
          d_in, key_lag, val_lag, sav_lead, out_lead, sol_lead, gram_in, state_in, cross_in, pair_in,
          r_s, p_s, y_s, rr_s, k2_s, kt_s, g_s, local_sem, send_sem, recv_sem):
     s = lax.axis_index("seq")
@@ -103,6 +103,12 @@
     tok = key.shape[0]
     w_copy = pltpu.make_async_copy(w_hbm, w, local_sem.at[0])
     x_copy = pltpu.make_async_copy(sav_hbm, sav, local_sem.at[1])
+    inputs = [
+        pltpu.make_async_copy(source, target, local_sem.at[2 + number])
+        for number, (source, target) in enumerate([(key_hbm, key), (d_hbm, d_own), (val_hbm, val)])
+    ]
+    for copy in inputs:
+        copy.start()
     w_copy.start()
     x_copy.start()
 
@@ -158,6 +164,8 @@
     def mids(source, target, sign):
         return [Hop(source, target.at[m - 1], sign * m).start() for m in range(1, span)]
 
+    for copy in inputs:
+        copy.wait()
     key_hop = Hop(key, key_lag, span).start()
     d_copies = []
     for j in range(1, n_head):
@@ -273,7 +281,7 @@
     copies = n_head - 1 + 5 + 4 * (span - 1)
     vmem = pl.BlockSpec(memory_space=pltpu.VMEM)
     smem = pl.BlockSpec(memory_space=pltpu.SMEM)
-    hbm = pl.BlockSpec(memory_space=pl.ANY)
+    hbm = pl.BlockSpec(memory_space=pltpu.HBM)
     flat = jax.ShapeDtypeStruct((tok, cols), F32)
     half = pltpu.VMEM((tok, cols), BF)
     mats = pltpu.VMEM((heads, DH, DH), BF)
@@ -283,9 +291,10 @@
         functools.partial(mega, span, n_seq, n_head),
         name="layer",
         out_shape=[flat, flat, flat],
-        in_specs=[smem, vmem, vmem, vmem, hbm, hbm],
+        in_specs=[smem, hbm, hbm, hbm, hbm, hbm],
         out_specs=[vmem, vmem, vmem],
         scratch_shapes=[
+            half, half, pltpu.VMEM(d_layer.shape, BF),
             pltpu.VMEM(out_weight.shape, BF), pltpu.VMEM((tok, cols), F32), half, half, half,
             mats, mats, mats, mats,
             pltpu.VMEM((n_head - 1,) + d_layer.shape, BF), half, half, half, half, half,
@@ -295,12 +304,12 @@
             pltpu.VMEM((heads, 2 * tok, 2 * DH), BF),
             pltpu.VMEM((heads, DH, 2 * tok), BF),
             pltpu.VMEM((heads, DH, 3 * DH), BF),
-            pltpu.SemaphoreType.DMA((2,)),
+            pltpu.SemaphoreType.DMA((5,)),
             pltpu.SemaphoreType.DMA((copies,)),
             pltpu.SemaphoreType.DMA((copies,)),
         ],
         compiler_params=pltpu.CompilerParams(
-            collective_id=0, has_side_effects=True, vmem_limit_bytes=40 << 20
+            collective_id=0, has_side_effects=True, vmem_limit_bytes=67043328
         ),
     )(ridge_scale, key_rows, values, d_layer, out_weight, saved_solutions)
 

time: 58 us -> 55 us (0.948)
  local copies, waits for them, and re-layouts: 8.51 us -> 4.59 us
  Pallas kernels: 48.5 us -> 49.6 us
    unnamed x15 -> x5, local copies, waits for them, and re-layouts: 8.51 us -> 4.59 us
    pallas_call x1, Pallas kernels: 48.5 us -> 49.6 us  [body(): pl.pallas_call(functools.partial(mega, span, n_seq, n_head), name='layer'...]
where the time goes in v1:
time: 55 us; the launch traced here: 54.8 us
  Pallas kernels  49.6 us (90%)
  local copies, waits for them, and re-layouts  4.59 us (8%)
  between operations  0.65 us (1%)
    pallas_call x1, Pallas kernels, body(): pl.pallas_call(functools.partial(mega, span, n_seq, n_head), name='layer'...  49.6 us
    unnamed x5, local copies, waits for them, and re-layouts  4.59 us

profile of v1, /device:TPU:11, one launch (start us, length us, event | category | flops | bytes accessed | tf_op | source)
XLA Modules:
  0.0 54.8 jit_solution(5219213870168799509)
XLA Ops:
  0.6 49.6 %layer.1 = (f32[256,512]{1,0:T(8,128)}, f32[256,512]{1,0:T(8,128)}, f32[256,512]{1,0:T(8,128)}) custom-call(f32[4]{0:T(128)} %ridge.1, bf16[256,512]{1,0:T(8,128)(2,1)} %key_hbm.1, bf16[256,512]{1,0:T(8,128)(2,1)} %val_hbm.1, bf16[256,512]{1,0:T(8,128)(2,1)} %d_hbm.1, bf16[512,2048]{1,0:T(8,128)(2,1)} %w_hbm.1, f32[256,512]{1,0:T(8,128)} %sav_hbm.1), custom_call_target="tpu_custom_call" | custom-call | tf_op jit(solution)/shard_map/layer/pallas_call | solution.py:290
  50.2 0.0 copy-start
  50.2 1.9 %copy.12 = f32[256,512]{1,0:T(8,128)} copy(f32[256,512]{1,0:T(8,128)} %get-tuple-element.6) | data formatting | bytes 1048576
  52.2 1.9 %copy.13 = f32[256,512]{1,0:T(8,128)} copy(f32[256,512]{1,0:T(8,128)} %get-tuple-element.7) | data formatting | bytes 1048576
  54.0 0.0 copy-done
  54.0 0.8 %copy.14 = f32[256,512]{1,0:T(8,128)} copy(f32[256,512]{1,0:T(8,128)S(1)} %copy-done) | data formatting | bytes 1048576
Async XLA Ops:
  50.2 3.8 %copy-start = (f32[256,512]{1,0:T(8,128)S(1)}, f32[256,512]{1,0:T(8,128)}, u32[]{:S(2)}) copy-start(f32[256,512]{1,0:T(8,128)} %get-tuple-element.8) | copy-start | bytes 1572868
